TPU v7x, 32 devices: a whole 2x2x4 slice. The times are simulated.
32 devices in a mesh: rep: 4 (over x, y), dp: 8 (over z, core).
Axes of the slice: x: 2, y: 2, z: 4, core: 2. Of those that a mesh axis runs over, the one named last changes fastest.
Arguments:
- x: bfloat16 [32, 2048, 768], P(('rep', 'dp')), parts along dimension 0
- dy: bfloat16 [32, 2048, 768], P(('rep', 'dp')), parts along dimension 0
- w_gate: bfloat16 [2, 768, 4480], replicated
- w_up: bfloat16 [2, 768, 4480], replicated
- w_down: bfloat16 [2, 4480, 768], replicated
- m_w_gate: float32 [2, 768, 4480], P(None, 'dp')
- m_w_up: float32 [2, 768, 4480], P(None, 'dp')
- m_w_down: float32 [2, 4480, 768], P(None, 'dp')
- v_w_gate: float32 [2, 768, 4480], P(None, 'dp')
- v_w_up: float32 [2, 768, 4480], P(None, 'dp')
- v_w_down: float32 [2, 4480, 768], P(None, 'dp')
Outputs:
- output 1: bfloat16 [8, 768, 4480], P('rep'), parts along dimension 0
- output 2: bfloat16 [8, 768, 4480], P('rep'), parts along dimension 0
- output 3: bfloat16 [8, 4480, 768], P('rep'), parts along dimension 0
- output 4: float32 [8, 768, 4480], P('rep', 'dp'), parts along dimension 0
- output 5: float32 [8, 768, 4480], P('rep', 'dp'), parts along dimension 0
- output 6: float32 [8, 4480, 768], P('rep', 'dp'), parts along dimension 0
- output 7: float32 [8, 768, 4480], P('rep', 'dp'), parts along dimension 0
- output 8: float32 [8, 768, 4480], P('rep', 'dp'), parts along dimension 0
- output 9: float32 [8, 4480, 768], P('rep', 'dp'), parts along dimension 0
There are 4 independent parts. A program takes and returns all parts, laid end to end along the dimension named above; an argument that names none is the same for every part.
All inputs are finite; a program needn't handle non-finite values.
Results may differ from a plain program's by a relative error of at most 0.022.
Values are sent between devices in bfloat16 or wider.
A program may use at most 2 GiB of HBM per device.

v0:
```python
import jax
import jax.numpy as jnp
from jax import lax

NAMES = ("w_gate", "w_up", "w_down")


def matmul(a, w):
    return jnp.dot(a, w, preferred_element_type=jnp.float32).astype(jnp.bfloat16)


def normed(h):
    wide = h.astype(jnp.float32)
    scale = lax.rsqrt(jnp.mean(wide**2, -1, keepdims=True) + 1e-6)
    return (wide * scale).astype(jnp.bfloat16)


def layer(h, w):
    a = normed(h)
    gate = jnp.dot(a, w["w_gate"], preferred_element_type=jnp.float32)
    up = jnp.dot(a, w["w_up"], preferred_element_type=jnp.float32)
    return h + matmul((jax.nn.silu(gate) * up).astype(jnp.bfloat16), w["w_down"])


def adamw(w, m, v, g):
    m = 0.9 * m + 0.1 * g
    v = 0.95 * v + 0.05 * g * g
    step = m * lax.rsqrt(v + 1e-8) + 0.1 * w
    return (w - 0.02 * step).astype(jnp.bfloat16), m, v


def clipped(gradients, sum_of_squares, count):
    factor = jnp.minimum(1.0, 0.5 * lax.rsqrt(sum_of_squares / count + 1e-30))
    return [g * factor for g in gradients]


def stack(weights, h):
    for number in range(weights["w_gate"].shape[0]):
        h = layer(h, {name: w[number] for name, w in weights.items()})
    return h


def solution(mesh):
    groups = mesh.shape["rep"]

    def step(x, dy, *arrays):
        weights, m, v = (arrays[i : i + 3] for i in (0, 3, 6))
        x, dy = (t.reshape(groups, -1, *t.shape[1:]) for t in (x, dy))

        def of_a_group(x, dy):
            _, back = jax.vjp(lambda w: stack(w, x), dict(zip(NAMES, weights, strict=True)))
            by_weights = back(dy)[0]
            gradients = [by_weights[name].astype(jnp.float32) for name in NAMES]
            gradients = clipped(gradients, sum(jnp.sum(g * g) for g in gradients), sum(g.size for g in gradients))
            new = [adamw(w.astype(jnp.float32), m, v, g) for w, m, v, g in zip(weights, m, v, gradients, strict=True)]
            return tuple(one[which] for which in range(3) for one in new)

        return tuple(t.reshape(-1, *t.shape[2:]) for t in jax.vmap(of_a_group)(x, dy))

    return step
```

profile of v0, /device:TPU:0, one launch (start us, length us, event | category | flops | bytes accessed | tf_op | source)
XLA Modules:
  0.0 1486.6 jit_solution(1615791740642926236)
XLA Ops:
  7.2 2.7 fusion.65
  10.0 4.6 copy
  14.6 22.3 %fusion.60 = f32[2048,4480]{1,0:T(8,128)} fusion(bf16[2,768,4480]{2,1,0:T(8,128)(2,1)} %param, bf16[1,2048,768]{2,1,0:T(8,128)(2,1)S(1)} %copy-done.1, f32[2048]{0:T(1024)S(1)} %add_rsqrt_fusion), kind=kOutput, calls=%fused_computation.71 | convolution fusion | flops 14097580032 | bytes 46735360 | tf_op jit(solution)/vmap(jvp())/dot_general | solution.py:20
  37.0 22.3 %fusion.58 = f32[2048,4480]{1,0:T(8,128)} fusion(bf16[2,768,4480]{2,1,0:T(8,128)(2,1)} %param.3, bf16[1,2048,768]{2,1,0:T(8,128)(2,1)S(1)} %copy-done.1, f32[2048]{0:T(1024)S(1)} %add_rsqrt_fusion), kind=kOutput, calls=%fused_computation.69 | convolution fusion | flops 14097580032 | bytes 46735360 | tf_op jit(solution)/vmap(jvp())/dot_general | solution.py:21
  59.3 30.7 %fusion.26 = bf16[2048,4480]{1,0:T(8,128)(2,1)} fusion(f32[2048,4480]{1,0:T(8,128)} %fusion.58, f32[2048,4480]{1,0:T(8,128)} %fusion.60), kind=kLoop, calls=%fused_computation.37 | loop fusion | flops 55050240 | bytes 91750400
  90.0 20.9 %fusion.69 = (f32[2048]{0:T(1024)S(1)}, bf16[1,1,2048,768]{2,3,1,0:T(8,128)(2,1)}) fusion(bf16[2048,4480]{1,0:T(8,128)(2,1)} %fusion.26, bf16[2,4480,768]{2,1,0:T(8,128)(2,1)} %param.4, bf16[1,2048,768]{1,2,0:T(8,128)(2,1)S(1)} %copy-done.5), kind=kOutput, calls=%fused_computation.80 | convolution fusion | flops 14100723712 | bytes 31531008 | tf_op jit(solution)/vmap(jvp())/dot_general | solution.py:9
  111.5 25.4 %fusion.47 = f32[2048,4480]{1,0:T(8,128)} fusion(bf16[2,768,4480]{2,1,0:T(8,128)(2,1)} %param, bf16[1,1,2048,768]{2,3,1,0:T(8,128)(2,1)} %get-tuple-element.10, f32[2048]{0:T(1024)S(1)} %bitcast.351), kind=kOutput, calls=%fused_computation.58 | convolution fusion | flops 14097580032 | bytes 46735360 | tf_op jit(solution)/vmap(jvp())/dot_general | solution.py:20
  136.9 25.2 %fusion.51 = f32[2048,4480]{1,0:T(8,128)} fusion(bf16[2,768,4480]{2,1,0:T(8,128)(2,1)} %param.3, bf16[1,1,2048,768]{2,3,1,0:T(8,128)(2,1)} %get-tuple-element.10, f32[2048]{0:T(1024)S(1)} %bitcast.352), kind=kOutput, calls=%fused_computation.62 | convolution fusion | flops 14097580032 | bytes 46735360 | tf_op jit(solution)/vmap(jvp())/dot_general | solution.py:21
  162.1 32.0 %fusion.35 = f32[1,4480,768]{2,1,0:T(8,128)} fusion(f32[2048,4480]{1,0:T(8,128)} %fusion.51, f32[2048,4480]{1,0:T(8,128)} %fusion.47, bf16[1,2048,768]{2,1,0:T(8,128)(2,1)S(1)} %copy-done.4), kind=kOutput, calls=%fused_computation.49 | convolution fusion | flops 14147911680 | bytes 90308608 | tf_op jit(solution)/vmap(transpose(jvp()))/dot_general | solution.py:9
  194.2 3.1 copy.1
  197.2 20.5 %convolution_convert_fusion.1 = bf16[2048,4480]{1,0:T(8,128)(2,1)} fusion(bf16[2,4480,768]{2,1,0:T(8,128)(2,1)} %param.4, bf16[1,2048,768]{2,1,0:T(8,128)(2,1)S(1)} %copy-done.4), kind=kOutput, calls=%fused_computation.36 | convolution fusion | flops 14102036480 | bytes 28377088 | tf_op jit(solution)/vmap(transpose(jvp()))/dot_general | solution.py:9
  217.8 35.7 %fusion.6 = bf16[2048,4480]{1,0:T(8,128)(2,1)} fusion(f32[2048,4480]{1,0:T(8,128)} %fusion.47, f32[2048,4480]{1,0:T(8,128)} %fusion.51, bf16[2048,4480]{1,0:T(8,128)(2,1)} %convolution_convert_fusion.1), kind=kLoop, calls=%fused_computation.11 | loop fusion | flops 110100480 | bytes 110100480
  253.5 25.4 %fusion.105 = bf16[2048,768]{0,1:T(8,128)(2,1)} fusion(bf16[2,768,4480]{2,1,0:T(8,128)(2,1)} %param.3, bf16[2048,4480]{1,0:T(8,128)(2,1)} %convolution_convert_fusion.1, f32[2048,4480]{1,0:T(8,128)} %fusion.47), kind=kOutput, calls=%fused_computation.132 | convolution fusion | flops 14149484544 | bytes 65077248 | tf_op jit(solution)/vmap(transpose(jvp()))/dot_general | solution.py:21
  279.0 24.0 %fusion.71 = (f32[2048]{0:T(1024)S(1)}, bf16[2048,768]{0,1:T(8,128)(2,1)}) fusion(bf16[1,1,2048,768]{2,3,1,0:T(8,128)(2,1)} %get-tuple-element.10, bf16[2048,768]{0,1:T(8,128)(2,1)} %fusion.105, bf16[2048,4480]{1,0:T(8,128)(2,1)} %fusion.6, bf16[2,768,4480]{2,1,0:T(8,128)(2,1)} %param), kind=kOutput, calls=%fused_computation.82 | convolution fusion | flops 14100723712 | bytes 34676736 | tf_op jit(solution)/vmap(transpose(jvp()))/dot_general | solution.py:20
  303.0 5.0 fusion.119
  308.1 1.7 copy-done.8
  309.7 20.4 %convolution_bitcast_fusion = f32[1,4480,768]{2,1,0:T(8,128)} fusion(bf16[2048,4480]{1,0:T(8,128)(2,1)} %fusion.26, bf16[2048,768]{0,1:T(8,128)(2,1)S(1)} %fusion.119), kind=kOutput, calls=%fused_computation.53 | convolution fusion | flops 14092861440 | bytes 35258368 | tf_op jit(solution)/vmap(transpose(jvp()))/dot_general | solution.py:9
  330.2 1.8 copy-done.7
  332.0 28.5 %fusion.38 = f32[1,768,4480]{2,1,0:T(8,128)} fusion(bf16[2048,4480]{1,0:T(8,128)(2,1)} %convolution_convert_fusion.1, f32[2048,4480]{1,0:T(8,128)} %fusion.47, bf16[1,1,2048,768]{2,3,1,0:T(8,128)(2,1)S(1)} %copy-done.7, f32[2048]{0:T(1024)S(1)} %bitcast.354), kind=kOutput, calls=%fused_computation.50 | convolution fusion | flops 14152630272 | bytes 71966720 | tf_op jit(solution)/vmap(transpose(jvp()))/dot_general | solution.py:21
  360.6 22.1 %convolution_convert_fusion = bf16[2048,4480]{1,0:T(8,128)(2,1)} fusion(bf16[2048,768]{0,1:T(8,128)(2,1)} %copy-done.8, bf16[2,4480,768]{2,1,0:T(8,128)(2,1)} %param.4), kind=kOutput, calls=%fused_computation.35 | convolution fusion | flops 14102036480 | bytes 28377088 | tf_op jit(solution)/vmap(transpose(jvp()))/dot_general | solution.py:9
  382.8 28.9 %fusion.44 = f32[1,768,4480]{2,1,0:T(8,128)} fusion(bf16[2048,4480]{1,0:T(8,128)(2,1)} %convolution_convert_fusion, f32[2048,4480]{1,0:T(8,128)} %fusion.60, bf16[1,2048,768]{1,2,0:T(8,128)(2,1)S(1)} %copy-done.6, f32[2048]{0:T(1024)S(1)} %copy-done.14), kind=kOutput, calls=%fused_computation.52 | convolution fusion | flops 14152630272 | bytes 71966720 | tf_op jit(solution)/vmap(transpose(jvp()))/dot_general | solution.py:21
  411.7 20.9 %convolution_bitcast_fusion.1 = f32[1,768,4480]{2,1,0:T(8,128)} fusion(bf16[2048,4480]{1,0:T(8,128)(2,1)} %fusion.6, bf16[1,1,2048,768]{2,3,1,0:T(8,128)(2,1)} %get-tuple-element.10, f32[2048]{0:T(1024)S(1)} %bitcast.355), kind=kOutput, calls=%fused_computation.54 | convolution fusion | flops 14097580032 | bytes 35266560 | tf_op jit(solution)/vmap(transpose(jvp()))/dot_general | solution.py:20
  432.7 37.9 %fusion.41 = f32[1,768,4480]{2,1,0:T(8,128)} fusion(f32[2048,4480]{1,0:T(8,128)} %fusion.60, f32[2048,4480]{1,0:T(8,128)} %fusion.58, bf16[2048,4480]{1,0:T(8,128)(2,1)} %convolution_convert_fusion, bf16[1,2048,768]{1,2,0:T(8,128)(2,1)S(1)} %copy-done.6, f32[2048]{0:T(1024)S(1)} %copy-done.14), kind=kOutput, calls=%fused_computation.51 | convolution fusion | flops 14198505472 | bytes 108666880 | tf_op jit(solution)/vmap(transpose(jvp()))/dot_general | solution.py:20
  472.5 1.5 convert_bitcast_fusion.4
  474.1 4.1 reduce-scatter.29.cloned.1.call-done
  478.2 1.5 convert_bitcast_fusion.3
  479.8 1.5 fusion.91
  481.3 138.1 %reduce-scatter.23.cloned.1.call-done = f32[1,96,4480]{2,1,0:T(8,128)} async-done(((f32[1,768,4480]{2,1,0:T(8,128)}), f32[1,96,4480]{2,1,0:T(8,128)}) %reduce-scatter.23.cloned.1.call-update) | async-done | bytes 1720336
  619.4 1.6 convert_bitcast_fusion.6
  620.9 140.0 %reduce-scatter.25.cloned.1.call-done = f32[1,96,4480]{2,1,0:T(8,128)} async-done(((f32[1,768,4480]{2,1,0:T(8,128)}), f32[1,96,4480]{2,1,0:T(8,128)}) %reduce-scatter.25.cloned.1.call-update) | async-done | bytes 1720336
  761.0 1.6 convert_bitcast_fusion.5
  762.5 1.5 fusion.90
  764.0 138.6 %reduce-scatter.19.cloned.1.call-done = f32[1,96,4480]{2,1,0:T(8,128)} async-done(((f32[1,768,4480]{2,1,0:T(8,128)}), f32[1,96,4480]{2,1,0:T(8,128)}) %reduce-scatter.19.cloned.1.call-update) | async-done | bytes 1720336
  902.6 2.5 convert_bitcast_fusion.8
  905.0 139.1 %reduce-scatter.21.cloned.1.call-done = f32[1,96,4480]{2,1,0:T(8,128)} async-done(((f32[1,768,4480]{2,1,0:T(8,128)}), f32[1,96,4480]{2,1,0:T(8,128)}) %reduce-scatter.21.cloned.1.call-update) | async-done | bytes 1720336
  1044.1 1.6 convert_bitcast_fusion.7
  1045.7 0.9 copy-done.3
  1046.6 2.7 fusion.89
  1051.2 14.9 %all-reduce.16 = f32[1]{0:T(128)} all-reduce(f32[1]{0:T(128)} %bitcast.50), channel_id=5, replica_groups=mesh['rep'=4,'dp'=8] {'dp'}, use_global_device_ids=true, to_apply=%region_3.4.clone | all-reduce | flops 1 | bytes 8 | tf_op jit(solution)/vmap()/reduce_sum | solution.py:54
  1066.8 6.6 fusion.137
  1073.5 6.9 fusion.139
  1080.5 6.6 fusion.138
  1087.1 110.9 %all-gather.14.cloned.1.call-done = bf16[1,2,4480,768]{3,2,1,0:T(8,128)(2,1)} async-done(((bf16[1,2,560,768]{3,2,1,0:T(8,128)(2,1)}), bf16[1,2,4480,768]{3,2,1,0:T(8,128)(2,1)}) %all-gather.14.cloned.1.call-update) | async-done | bytes 13762576 | tf_op jit(solution)/reshape | solution.py:58
  1198.0 127.0 %all-gather.10.cloned.1.call-done = bf16[1,2,768,4480]{3,2,1,0:T(8,128)(2,1)} async-done(((bf16[1,2,96,4480]{3,2,1,0:T(8,128)(2,1)}), bf16[1,2,768,4480]{3,2,1,0:T(8,128)(2,1)}) %all-gather.10.cloned.1.call-update) | async-done | bytes 13762576 | tf_op jit(solution)/reshape | solution.py:58
  1325.0 127.0 %all-gather.12.cloned.1.call-done = bf16[1,2,768,4480]{3,2,1,0:T(8,128)(2,1)} async-done(((bf16[1,2,96,4480]{3,2,1,0:T(8,128)(2,1)}), bf16[1,2,768,4480]{3,2,1,0:T(8,128)(2,1)}) %all-gather.12.cloned.1.call-update) | async-done | bytes 13762576 | tf_op jit(solution)/reshape | solution.py:58
  1452.0 15.3 %copy.5 = bf16[2,768,4480]{2,1,0:T(8,128)(2,1)} copy(bf16[2,768,4480]{2,1,0:T(8,128)(2,1)} %bitcast.346) | data formatting | bytes 27525120
  1467.3 6.6 copy.6
  1474.5 5.2 copy.7
  (62 shorter events, 3.0 us)
Async XLA Ops:
  7.2 7.4 copy-start.1
  7.2 465.3 %reduce-scatter.27.cloned.1.call-start = ((), (), s32[]{:S(2)}) async-start(), calls=%async_computation.13 | async-start | bytes 15482880
  14.6 22.4 %copy-start.13 = (f32[2048]{0:T(1024)}, f32[2048]{0:T(1024)S(1)}, u32[]{:S(2)}) copy-start(f32[2048]{0:T(1024)S(1)} %add_rsqrt_fusion) | copy-start | bytes 24580
  59.3 30.7 %copy-start.5 = (bf16[1,2048,768]{1,2,0:T(8,128)(2,1)S(1)}, bf16[1,2048,768]{1,2,0:T(8,128)(2,1)}, u32[]{:S(2)}) copy-start(bf16[1,2048,768]{1,2,0:T(8,128)(2,1)} %copy) | copy-start | bytes 9437188
  110.9 0.6 copy-start.9
  111.5 25.4 %copy-start.11 = (f32[1,1,2048]{2,1,0:T(1,128)}, f32[1,1,2048]{2,1,0:T(1,128)S(1)}, u32[]{:S(2)}) copy-start(f32[1,1,2048]{2,1,0:T(1,128)S(1)} %rsqrt.38) | copy-start | bytes 24580
  136.9 25.2 %copy-start.4 = (bf16[1,2048,768]{2,1,0:T(8,128)(2,1)S(1)}, bf16[1,2048,768]{2,1,0:T(8,128)(2,1)}, u32[]{:S(2)}) copy-start(bf16[1,2048,768]{2,1,0:T(8,128)(2,1)} %param.5) | copy-start | bytes 9437188
  194.1 284.1 %reduce-scatter.29.cloned.1.call-start = ((), (), s32[]{:S(2)}) async-start(), calls=%async_computation.14 | async-start | bytes 15482880
  278.9 24.0 %copy-start.10 = (f32[2048]{0:T(1024)S(1)}, f32[2048]{0:T(1024)}, u32[]{:S(2)}) copy-start(f32[2048]{0:T(1024)} %copy-done.9) | copy-start | bytes 24580
  278.9 24.1 %copy-start.2 = (bf16[1,2048,768]{1,2,0:T(8,128)(2,1)S(1)}, bf16[1,2048,768]{1,2,0:T(8,128)(2,1)}, u32[]{:S(2)}) copy-start(bf16[1,2048,768]{1,2,0:T(8,128)(2,1)} %copy.1) | copy-start | bytes 9437188
  278.9 24.1 %copy-start.12 = (f32[1,1,2048]{2,1,0:T(1,128)S(1)}, f32[1,1,2048]{2,1,0:T(1,128)}, u32[]{:S(2)}) copy-start(f32[1,1,2048]{2,1,0:T(1,128)} %copy-done.11) | copy-start | bytes 24580
  308.1 1.7 copy-start.8
  330.1 1.9 copy-start.7
  330.2 289.2 %reduce-scatter.23.cloned.1.call-start = ((), (), s32[]{:S(2)}) async-start(), calls=%async_computation.11 | async-start | bytes 15482880
  360.6 22.2 %copy-start.6 = (bf16[1,2048,768]{1,2,0:T(8,128)(2,1)S(1)}, bf16[1,2048,768]{1,2,0:T(8,128)(2,1)}, u32[]{:S(2)}) copy-start(bf16[1,2048,768]{1,2,0:T(8,128)(2,1)} %copy) | copy-start | bytes 9437188
  360.6 22.2 %copy-start.14 = (f32[2048]{0:T(1024)S(1)}, f32[2048]{0:T(1024)}, u32[]{:S(2)}) copy-start(f32[2048]{0:T(1024)} %copy-done.13) | copy-start | bytes 24580
  360.6 400.4 %reduce-scatter.25.cloned.1.call-start = ((), (), s32[]{:S(2)}) async-start(), calls=%async_computation.12 | async-start | bytes 15482880
  411.7 490.9 %reduce-scatter.19.cloned.1.call-start = ((), (), s32[]{:S(2)}) async-start(), calls=%async_computation.9 | async-start | bytes 15482880
  432.7 611.4 %reduce-scatter.21.cloned.1.call-start = ((), (), s32[]{:S(2)}) async-start(), calls=%async_computation.10 | async-start | bytes 15482880
  470.6 0.7 copy-start.15
  470.6 727.3 %all-gather.14.cloned.1.call-start = ((), (), s32[]{:S(2)}) async-start(), calls=%async_computation.8 | async-start | bytes 15482880 | tf_op jit(solution)/reshape | solution.py:58
  1045.7 0.9 copy-start.3
  1073.5 251.5 %all-gather.10.cloned.1.call-start = ((), (), s32[]{:S(2)}) async-start(), calls=%async_computation.6 | async-start | bytes 15482880 | tf_op jit(solution)/reshape | solution.py:58
  1080.4 371.6 %all-gather.12.cloned.1.call-start = ((), (), s32[]{:S(2)}) async-start(), calls=%async_computation.7 | async-start | bytes 15482880 | tf_op jit(solution)/reshape | solution.py:58
  1452.0 15.3 %copy-start = (bf16[1,2,768,4480]{3,2,1,0:T(8,128)(2,1)S(1)}, bf16[1,2,768,4480]{3,2,1,0:T(8,128)(2,1)}, u32[]{:S(2)}) copy-start(bf16[1,2,768,4480]{3,2,1,0:T(8,128)(2,1)} %all-gather.12.cloned.1.call-done) | copy-start | bytes 41287684
  1452.0 21.9 %slice-start = ((s8[13762560]{0:T(1024)(128)(4,1)}), s8[4194304]{0:T(1024)(128)(4,1)S(1)}, s32[]{:S(2)}) async-start(s8[13762560]{0:T(1024)(128)(4,1)} %bitcast.343), calls=%async_computation.15 | async-start | bytes 8388608
  1452.0 21.9 %slice-start.1 = ((s8[13762560]{0:T(1024)(128)(4,1)}), s8[4194304]{0:T(1024)(128)(4,1)S(1)}, s32[]{:S(2)}) async-start(s8[13762560]{0:T(1024)(128)(4,1)} %bitcast.343), calls=%async_computation.16 | async-start | bytes 8388608
  1467.3 6.7 slice-start.2
  1467.3 7.2 slice-start.3
Sparse Core Ops, SparseCore 0:
  194.2 142.8 reduce-scatter.26
  339.4 138.7 reduce-scatter.28
  480.5 138.7 reduce-scatter.22
  622.1 138.7 reduce-scatter.24
  763.7 138.8 reduce-scatter.18
  905.3 138.7 reduce-scatter.20
  1073.6 124.3 all-gather.13
  1200.1 124.7 all-gather.9
  1327.2 124.7 all-gather.11
where the time goes:
time: 1500 us; the launch traced here: 1490 us
  waiting for transfers between devices  925 us (62%)
  matrix products  377 us (25%)
  other arithmetic  110 us (7%)
  local copies, waits for them, and re-layouts  41.5 us (3%)
  between operations  17.7 us (1%)
    unnamed x15, waiting for transfers between devices  560 us
    reshape x3, waiting for transfers between devices, step(): t.reshape(-1, *t.shape[2:])  365 us
    dot_general x5, matrix products, layer(): gate = jnp.dot(a, w['w_gate'], preferred_element_type=jnp.float32)  131 us
    dot_general x5, matrix products, layer(): up = jnp.dot(a, w['w_up'], preferred_element_type=jnp.float32)  130 us
    dot_general x5, matrix products, matmul(): jnp.dot(a, w, preferred_element_type=jnp.float32).astype(jnp.bfloat16)  116 us
    unnamed x4, other arithmetic  71.5 us
    unnamed x45, local copies, waits for them, and re-layouts  40.9 us
  transfers between devices with their start and end apart: 9, of which 8 were waited for; matrix products, arithmetic and copies ran while one was open for 20% of the time, Pallas kernels for 0%

commit v1 on v0

v1 whole, which is shorter than its diff:
```python
import functools

import jax
import jax.numpy as jnp
from jax import lax
from jax.experimental import pallas as pl
from jax.experimental.pallas import tpu as pltpu
from jax.sharding import PartitionSpec as P

MESH = pl.DeviceIdType.MESH
f32, bf16 = jnp.float32, jnp.bfloat16
T, D, F = 2048, 768, 4480
BF = 640
NB = F // BF
TC = 512
HD = 384
HB = 320
GRP, DOWN = 96, 560


def sig(x):
    return 0.5 * jnp.tanh(0.5 * x) + 0.5

def ka_kernel(x_ref, wg_ref, wu_ref, wd_ref, h_ref, a_s, w_s, wd_s, hid_s, sems, wd_sem, *, layer):
    def fetch(j):
        s = j % 2
        c = pl.ds(pl.multiple_of(j * BF, 128), BF)
        return (pltpu.make_async_copy(wg_ref.at[layer, :, c], w_s.at[s, :, pl.ds(0, BF)], sems.at[s, 0]),
                pltpu.make_async_copy(wu_ref.at[layer, :, c], w_s.at[s, :, pl.ds(BF, BF)], sems.at[s, 1]))
    for c in fetch(0): c.start()
    wdc = pltpu.make_async_copy(wd_ref.at[layer], wd_s, wd_sem)
    def norm(r, _):
        rows = pl.ds(pl.multiple_of(r * TC, TC), TC)
        wide = x_ref[rows, :].astype(jnp.float32)
        scale = lax.rsqrt(jnp.mean(wide * wide, -1, keepdims=True) + 1e-6)
        a_s[rows, :] = (wide * scale).astype(jnp.bfloat16)
        return _
    lax.fori_loop(0, T // TC, norm, 0)
    def block(j, z):
        s = lax.rem(j, 2)
        @pl.when(j + 1 < NB)
        def _():
            for c in fetch(j + 1): c.start()
        @pl.when(j == 0)
        def _(): wdc.start()
        for c in fetch(j): c.wait()
        def rowsf(r, _):
            rows = pl.ds(pl.multiple_of(r * TC, TC), TC)
            gu = jnp.dot(a_s[rows, :], w_s[s], preferred_element_type=jnp.float32)
            gate, up = gu[:, :BF], gu[:, BF:]
            hid_s[rows, pl.ds(pl.multiple_of(j * BF, 128), BF)] = (gate * sig(gate) * up).astype(jnp.bfloat16)
            return _
        lax.fori_loop(0, T // TC, rowsf, 0)
        return z
    lax.fori_loop(0, NB, block, 0)
    wdc.wait()
    def down(r, _):
        rows = pl.ds(pl.multiple_of(r * TC, TC), TC)
        y = jnp.dot(hid_s[rows, :], wd_s[...], preferred_element_type=jnp.float32).astype(jnp.bfloat16)
        h_ref[rows, :] = x_ref[rows, :] + y
        return _
    lax.fori_loop(0, T // TC, down, 0)

def ka(x, wg, wu, wd, layer=0):
    V = pl.BlockSpec(memory_space=pltpu.VMEM); A = pl.BlockSpec(memory_space=pl.ANY)
    return pl.pallas_call(functools.partial(ka_kernel, layer=layer), out_shape=jax.ShapeDtypeStruct((T, D), jnp.bfloat16),
        in_specs=[V, A, A, A], out_specs=V,
        scratch_shapes=[pltpu.VMEM((T, D), jnp.bfloat16), pltpu.VMEM((2, D, 2 * BF), jnp.bfloat16), pltpu.VMEM((F, D), jnp.bfloat16),
                        pltpu.VMEM((T, F), jnp.bfloat16), pltpu.SemaphoreType.DMA((2, 2)), pltpu.SemaphoreType.DMA],
        compiler_params=pltpu.CompilerParams(vmem_limit_bytes=60 << 20), name="ka")(x, wg, wu, wd)


RING = 4


def block_of(i):
    return jnp.where(i % 2 == 0, i // 2, NB - 1 - i // 2)

def lkernel(h_ref, dh_ref, wg_ref, wu_ref, wd_ref, *rest, layer, with_da, comm):
    if with_da:
        dho_ref, *rest = rest
    (guf_ref, df_ref, ss_ref, a_s, w_s, wd_s, hid_s, dgu_s, bgu, bd, sgu, sd, igu, idd, ss_s, *rest) = rest
    if with_da:
        da_s, *rest = rest
    (wsem, rgu, rd, sendgu, sendd, d2dgu_s, d2dd_s, d2dgu_r, d2dd_r, fsem_gu, fsem_d, cred) = rest
    me = lax.axis_index("dp")
    chip = me // 2
    core = me % 2
    sib = me + 1 - 2 * core
    pos = (3 - chip, chip)
    nxt = (me - 2, me + 2)

    def rdma(src, dst, ssem, rsem, dev):
        return pltpu.make_async_remote_copy(src, dst, ssem, rsem, device_id={"dp": dev}, device_id_type=MESH)

    if comm:
        bar = pltpu.get_barrier_semaphore()
        pl.semaphore_signal(bar, inc=1, device_id={"dp": sib}, device_id_type=MESH)
        @pl.when(chip > 0)
        def _(): pl.semaphore_signal(bar, inc=1, device_id={"dp": me - 2}, device_id_type=MESH)
        @pl.when(chip < 3)
        def _(): pl.semaphore_signal(bar, inc=1, device_id={"dp": me + 2}, device_id_type=MESH)

    def fetch(i):
        s = i % 2
        b = block_of(i)
        c = pl.ds(pl.multiple_of(b * BF, 128), BF)
        return (pltpu.make_async_copy(wg_ref.at[layer, :, c], w_s.at[s, :, pl.ds(0, BF)], wsem.at[s, 0]),
                pltpu.make_async_copy(wu_ref.at[layer, :, c], w_s.at[s, :, pl.ds(BF, BF)], wsem.at[s, 1]),
                pltpu.make_async_copy(wd_ref.at[layer, c, :], wd_s.at[s], wsem.at[s, 2]))
    for c in fetch(0): c.start()

    def norm(r, z):
        rows = pl.ds(pl.multiple_of(r * TC, TC), TC)
        wide = h_ref[rows, :].astype(f32)
        scale = lax.rsqrt(jnp.mean(wide * wide, -1, keepdims=True) + 1e-6)
        a_s[rows, :] = (wide * scale).astype(bf16)
        if with_da:
            da_s[rows, :] = jnp.zeros((TC, D), f32)
        return z
    lax.fori_loop(0, T // TC, norm, 0)
    ss_s[...] = jnp.zeros_like(ss_s)
    if comm:
        pl.semaphore_wait(bar, 1 + (chip > 0).astype(jnp.int32) + (chip < 3).astype(jnp.int32))

    def d2d_gu(i):
        return rdma(bgu.at[RING], sgu.at[i % RING], d2dgu_s, d2dgu_r.at[i % RING], sib)
    def d2d_d(i):
        return rdma(bd.at[RING], sd.at[i % RING], d2dd_s, d2dd_r.at[i % RING], sib)
    def msg_gu(i, d):
        return rdma(bgu.at[i % RING, pl.ds(2 * d, 2)], igu.at[d, i], sendgu.at[i % RING, d], rgu.at[d, i], nxt[d])
    def msg_d(i, h, d):
        return rdma(bd.at[i % RING, h], idd.at[i, h], sendd.at[i % RING, h], rd.at[i, h], nxt[d])
    def fin_gu(i, d):
        return pltpu.make_async_copy(bgu.at[i % RING, pl.ds(2 * d, 2)], guf_ref.at[block_of(i)], fsem_gu.at[i % RING])
    def fin_d(i, h, d):
        return pltpu.make_async_copy(bd.at[i % RING, h], df_ref.at[2 * block_of(i) + h - (NB if d else 0)], fsem_d.at[i % RING, h])

    def add(own, sibv, inc, n, width, p):
        def go(r, z, first, last):
            rows = pl.ds(pl.multiple_of(r * 32, 32), 32)
            total = own[rows, :].astype(f32) + sibv[rows, :].astype(f32)
            if not first:
                total = total + inc[rows, :].astype(f32)
            out = total.astype(bf16)
            own[rows, :] = out
            if last:
                sq = out.astype(f32)
                ss_s[:, :width] += sq * sq
            return z
        for first, last, cond in ((True, False, p == 0), (False, False, (p > 0) & (p < 3)), (False, True, p == 3)):
            @pl.when(cond)
            def _(): lax.fori_loop(0, n // 32, functools.partial(go, first=first, last=last), 0)

    def process_gu(s):
        for d in (0, 1):
            p = pos[d]
            i = s - 1 - p
            @pl.when((i >= 0) & (i < NB))
            def _():
                if d == 0:
                    pass
                @pl.when(p > 0)
                def _(): msg_gu(i, d).wait_recv()
                for k in (0, 1):
                    add(bgu.at[i % RING, 2 * d + k], sgu.at[i % RING, 2 * d + k], igu.at[d, i, k], GRP, 2 * BF, p)
                @pl.when(p < 3)
                def _(): msg_gu(i, d).start()
                @pl.when(p == 3)
                def _(): fin_gu(i, d).start()

    def process_d(s):
        for d in (0, 1):
            p = pos[d]
            i = s - p
            for h in (0, 1):
                mine = jnp.where(i == NB - 1, h == d, i % 2 == d)
                @pl.when((i >= 0) & (i < NB) & mine)
                def _():
                    @pl.when(p > 0)
                    def _(): msg_d(i, h, d).wait_recv()
                    add(bd.at[i % RING, h], sd.at[i % RING, h], idd.at[i, h], HB, HD, p)
                    @pl.when(p < 3)
                    def _(): msg_d(i, h, d).start()
                    @pl.when(p == 3)
                    def _(): fin_d(i, h, d).start()

    def settle_gu(i):
        for d in (0, 1):
            @pl.when(pos[d] < 3)
            def _(): msg_gu(i, d).wait_send()
            @pl.when(pos[d] == 3)
            def _(): fin_gu(i, d).wait()
    def settle_d(i):
        for d in (0, 1):
            for h in (0, 1):
                mine = jnp.where(i == NB - 1, h == d, i % 2 == d)
                @pl.when(mine & (pos[d] < 3))
                def _(): msg_d(i, h, d).wait_send()
                @pl.when(mine & (pos[d] == 3))
                def _(): fin_d(i, h, d).wait()

    def wait_sib_gu(i):
        @pl.when((i >= 0) & (i < NB))
        def _(): d2d_gu(i).wait_recv()
    def wait_sib_d(i):
        @pl.when((i >= 0) & (i < NB))
        def _(): d2d_d(i).wait_recv()

    def step(s, z):
        w = lax.rem(s, 2)
        @pl.when(s < NB)
        def _():
            @pl.when(s + 1 < NB)
            def _():
                for c in fetch(s + 1): c.start()
            for c in fetch(s): c.wait()
            def ff(r, zz):
                rows = pl.ds(pl.multiple_of(r * TC, TC), TC)
                gu = jnp.dot(a_s[rows, :], w_s[w], preferred_element_type=f32)
                dhid = lax.dot_general(dh_ref[rows, :], wd_s[w], (((1,), (1,)), ((), ())), preferred_element_type=f32).astype(bf16).astype(f32)
                gate, up = gu[:, :BF], gu[:, BF:]
                sg = sig(gate)
                silu = gate * sg
                hid_s[rows, :] = (silu * up).astype(bf16)
                dgu_s[rows, BF:] = (dhid * silu).astype(bf16)
                dgu_s[rows, :BF] = (dhid * up * (sg + silu * (1.0 - sg))).astype(bf16)
                return zz
            lax.fori_loop(0, T // TC, ff, 0)
            if comm:
                @pl.when(s >= RING)
                def _(): settle_d(s - RING)
                @pl.when(s >= 1)
                def _(): d2d_d(s - 1).wait_send()
            g = lax.dot_general(hid_s[...], dh_ref[...], (((0,), (0,)), ((), ())), preferred_element_type=f32).astype(bf16)
            for q in (0, 1):
                idx = jnp.where(core == q, s % RING, RING)
                for h in (0, 1):
                    bd[idx, h] = g[HB * h:HB * (h + 1), HD * q:HD * (q + 1)]
            if comm:
                @pl.when(s >= RING)
                def _(): pl.semaphore_wait(cred.at[0], 1)
                d2d_d(s).start()
        if comm:
            wait_sib_gu(s - 1)
            process_gu(s)
            @pl.when((s >= 4) & (s < NB))
            def _(): pl.semaphore_signal(cred.at[1], 1, device_id={"dp": sib}, device_id_type=MESH)
        @pl.when(s < NB)
        def _():
            if comm:
                @pl.when(s >= RING)
                def _(): settle_gu(s - RING)
                @pl.when(s >= 1)
                def _(): d2d_gu(s - 1).wait_send()
            for half in (0, 1):
                g = lax.dot_general(a_s[:, HD * half:HD * (half + 1)], dgu_s[...], (((0,), (0,)), ((), ())), preferred_element_type=f32).astype(bf16)
                for pp in range(4):
                    k, q = (4 * half + pp) // 2, pp % 2
                    idx = jnp.where(core == q, s % RING, RING)
                    bgu[idx, k] = g[GRP * pp:GRP * (pp + 1), :]
            if comm:
                @pl.when(s >= RING)
                def _(): pl.semaphore_wait(cred.at[1], 1)
                d2d_gu(s).start()
        if comm:
            wait_sib_d(s)
            process_d(s)
            @pl.when((s >= 3) & (s < NB - 1))
            def _(): pl.semaphore_signal(cred.at[0], 1, device_id={"dp": sib}, device_id_type=MESH)
        if with_da:
            @pl.when(s < NB)
            def _():
                def dac(r, zz):
                    rows = pl.ds(pl.multiple_of(r * TC, TC), TC)
                    da_s[rows, :] += lax.dot_general(dgu_s[rows, :], w_s[w], (((1,), (1,)), ((), ())), preferred_element_type=f32)
                    return zz
                lax.fori_loop(0, T // TC, dac, 0)
                @pl.when(s == NB - 1)
                def _():
                    def nb(r, zz):
                        rows = pl.ds(pl.multiple_of(r * TC, TC), TC)
                        da = da_s[rows, :].astype(bf16).astype(f32)
                        wide = h_ref[rows, :].astype(f32)
                        scale = lax.rsqrt(jnp.mean(wide * wide, -1, keepdims=True) + 1e-6)
                        dscale = jnp.sum(da * wide, -1, keepdims=True)
                        c = dscale * (-1.0 / D) * (scale * scale * scale)
                        dho_ref[rows, :] = dh_ref[rows, :] + (da * scale + wide * c).astype(bf16)
                        return zz
                    lax.fori_loop(0, T // TC, nb, 0)
        return z
    lax.fori_loop(0, NB + 4 if comm else NB, step, 0)
    if comm:
        d2d_d(NB - 1).wait_send()
        d2d_gu(NB - 1).wait_send()
        for i in range(NB - RING, NB):
            settle_d(jnp.int32(i))
            settle_gu(jnp.int32(i))
    ss_ref[...] = jnp.full(ss_ref.shape, jnp.sum(ss_s[...]), f32)

def lcall(h, dh, wg, wu, wd, *, layer, with_da, comm=True):
    V = pl.BlockSpec(memory_space=pltpu.VMEM); A = pl.BlockSpec(memory_space=pl.ANY)
    S = jax.ShapeDtypeStruct
    outs = [S((NB, 2, GRP, 2 * BF), bf16), S((NB, HB, HD), bf16), S((8, 128), f32)]
    ospec = [A, A, V]
    if with_da:
        outs = [S((T, D), bf16)] + outs; ospec = [V] + ospec
    DMA = pltpu.SemaphoreType.DMA
    scratch = [pltpu.VMEM((T, D), bf16), pltpu.VMEM((2, D, 2 * BF), bf16), pltpu.VMEM((2, BF, D), bf16), pltpu.VMEM((T, BF), bf16), pltpu.VMEM((T, 2 * BF), bf16),
               pltpu.VMEM((RING + 1, 4, GRP, 2 * BF), bf16), pltpu.VMEM((RING + 1, 2, HB, HD), bf16), pltpu.VMEM((RING, 4, GRP, 2 * BF), bf16), pltpu.VMEM((RING, 2, HB, HD), bf16),
               pltpu.VMEM((2, NB, 2, GRP, 2 * BF), bf16), pltpu.VMEM((NB, 2, HB, HD), bf16), pltpu.VMEM((32, 2 * BF), f32)]
    if with_da: scratch.append(pltpu.VMEM((T, D), f32))
    scratch += [DMA((2, 3)), DMA((2, NB)), DMA((NB, 2)), DMA((RING, 2)), DMA((RING, 2)), DMA, DMA, DMA((RING,)), DMA((RING,)), DMA((RING,)), DMA((RING, 2)), pltpu.SemaphoreType.REGULAR((2,))]
    return pl.pallas_call(functools.partial(lkernel, layer=layer, with_da=with_da, comm=comm), out_shape=outs, in_specs=[V, V, A, A, A], out_specs=ospec,
        scratch_shapes=scratch, name=f"back{layer}",
        compiler_params=pltpu.CompilerParams(vmem_limit_bytes=67_000_000, **(dict(collective_id=layer, has_side_effects=True) if comm else {})))(h, dh, wg, wu, wd)


GR, DR = 32, 112
NG, ND = GRP // GR, DOWN // DR
MG = 4 * NG
NM = MG + 2 * ND
WS = 4
COUNT = 6 * D * F

def kc_kernel(gu1_ref, gu0_ref, d1_ref, d0_ref, ss_ref, wg, wu, wd, mg, mu, md, vg, vu, vd,
              nwg, nwu, nwd, nmg, nmu, nmd, nvg, nvu, nvd,
              ggu, gd, mb, vb, wb, mo, vo, wo, mbd, vbd, wbd, mod, vod, wod, ssr,
              lsem, rgu, rd, fgu, fd, psem, osem, wsem, rsem, relay_send, relay_sib, sibr, ssend, srecv):
    me = lax.axis_index("dp")
    chip = me // 2
    core = me % 2
    sib = me + 1 - 2 * core
    end = (chip == 0) | (chip == 3)
    guf, df = (gu0_ref, gu1_ref), (d0_ref, d1_ref)
    nw, w, m, v, nm, nv = (nwg, nwu, nwd), (wg, wu, wd), (mg, mu, md), (vg, vu, vd), (nmg, nmu, nmd), (nvg, nvu, nvd)

    def rdma(src, dst, ssem, rsem_, dev):
        return pltpu.make_async_remote_copy(src, dst, ssem, rsem_, device_id={"dp": dev}, device_id_type=MESH)

    kk = jnp.where(chip == 0, 0, 1)
    def own_g():
        out = []
        for l in (0, 1):
            out.append(pltpu.make_async_copy(guf[l].at[:, kk], ggu.at[l], lsem.at[2 * l]))
            out.append(pltpu.make_async_copy(df[l].at[pl.ds(pl.multiple_of(DOWN * (me % 4), 16), DOWN), :], gd.at[l, core], lsem.at[2 * l + 1]))
        return out
    @pl.when(end)
    def _():
        for c in own_g(): c.start()

    def parts(r):
        q = r // NG
        rd_ = r - MG
        return q // 2, q % 2, (r % NG) * GR, rd_ // ND, (rd_ % ND) * DR
    def each(r, fn):
        lg, mat, rg, ld, rdn = parts(r)
        for k in (0, 1):
            @pl.when((r < MG) & (mat == k))
            def _(): fn(k, lg, pl.multiple_of(rg, 16), GR)
        @pl.when(r >= MG)
        def _(): fn(2, ld, pl.multiple_of(rdn, 16), DR)

    def fetch(r):
        s = r % 2
        def fn(k, l, row, rows):
            def go():
                a, b, c = (mbd, vbd, wbd) if k == 2 else (mb, vb, wb)
                first = me * (DOWN if k == 2 else GRP) + row
                return (pltpu.make_async_copy(m[k].at[l, pl.ds(row, rows), :], a.at[s], psem.at[s, 0]),
                        pltpu.make_async_copy(v[k].at[l, pl.ds(row, rows), :], b.at[s], psem.at[s, 1]),
                        pltpu.make_async_copy(w[k].at[l, pl.ds(pl.multiple_of(first, 16), rows), :], c.at[s], psem.at[s, 2]))
            return go()
        return fn
    def start_fetch(r):
        def fn(*a):
            for c in fetch(r)(*a): c.start()
        each(r, fn)
    start_fetch(jnp.int32(0))

    bar = pltpu.get_barrier_semaphore()
    for t in range(1, 8):
        pl.semaphore_signal(bar, inc=1, device_id={"dp": lax.rem(me + t, 8)}, device_id_type=MESH)
    pl.semaphore_wait(bar, 7)

    slot = core + 2 * (me // 4)
    def ss_copy(t):
        return rdma(ss_ref, ssr.at[slot], ssend.at[t], srecv.at[slot], jnp.int32(t))
    @pl.when(end)
    def _():
        for t in range(8):
            @pl.when(me != t)
            def _(): ss_copy(t).start()

    def fwd_gu(r):
        k2 = 1 - kk
        out = []
        lg, mat, rg, _, _ = parts(r)
        rows = pl.ds(pl.multiple_of(rg, 16), GR)
        cols = pl.ds(pl.multiple_of(mat * BF, 128), BF)
        dev = jnp.where(chip == 0, me + 2, me - 2)
        for l in (0, 1):
            out.append((lg == l, rdma(guf[l].at[:, k2, rows, cols], ggu.at[l, :, rows, cols], fgu.at[r % 2], rgu.at[r], dev)))
        return out
    def fwd_d(r, q):
        _, _, _, ld, rdn = parts(r)
        dev = 4 * (me // 4) + q
        out = []
        for l in (0, 1):
            out.append(((ld == l) & (dev != me), rdma(df[l].at[pl.ds(pl.multiple_of(DOWN * q + rdn, 16), DR), :], gd.at[l, core, pl.ds(pl.multiple_of(rdn, 16), DR), :],
                        fd.at[q, r % 2], rd.at[r - MG, core], dev)))
        return out
    def forward(r):
        @pl.when(end & (r < MG))
        def _():
            for l, (cond, c) in enumerate(fwd_gu(r)):
                @pl.when(cond)
                def _(): c.start()
        @pl.when(end & (r >= MG) & (r < NM))
        def _():
            for q in range(4):
                for cond, c in fwd_d(r, q):
                    @pl.when(cond)
                    def _(): c.start()
    def forward_done(r):
        @pl.when(end & (r >= 0) & (r < MG))
        def _():
            for cond, c in fwd_gu(r):
                @pl.when(cond)
                def _(): c.wait_send()
        @pl.when(end & (r >= MG) & (r < NM))
        def _():
            for q in range(4):
                for cond, c in fwd_d(r, q):
                    @pl.when(cond)
                    def _(): c.wait_send()
    LEAD = 2
    for r in range(LEAD): forward(jnp.int32(r))

    @pl.when(end)
    def _():
        for c in own_g(): c.wait()
    total = jnp.zeros((8, 128), f32)
    for s, dev in enumerate((0, 1, 6, 7)):
        @pl.when(me != dev)
        def _(): rdma(ss_ref, ssr.at[s], ssend.at[0], srecv.at[s], jnp.int32(dev)).wait_recv()
        total += jnp.where(me == dev, ss_ref[...], ssr[s])
    factor = jnp.minimum(1.0, 0.5 * lax.rsqrt(total / COUNT + 1e-30))[0:1, 0:1]

    def adamw(wv, mv, vv, g):
        g = g.astype(f32) * factor
        mn = 0.9 * mv + 0.1 * g
        vn = 0.95 * vv + 0.05 * g * g
        wv = wv.astype(f32)
        return (wv - 0.02 * (mn * lax.rsqrt(vn + 1e-8) + 0.1 * wv)).astype(bf16), mn, vn

    def place(k, dev, l, row, rows):
        first = dev * (DOWN if k == 2 else GRP) + row
        return nw[k].at[l, pl.ds(pl.multiple_of(first, 16), rows), :]
    def own_w(r, k, l, row, rows):
        s = r % WS
        src = (wod if k == 2 else wo).at[s]
        dst = place(k, me, l, row, rows)
        return (lambda: pltpu.make_async_copy(src, dst, wsem.at[s, 0]),
                lambda: rdma(src, dst, wsem.at[s, 1], rsem.at[0, 0, r], me + 2),
                lambda: rdma(src, dst, wsem.at[s, 2], rsem.at[1, 0, r], me - 2),
                lambda: rdma(src, dst, wsem.at[s, 3], sibr.at[k], sib))
    def own_mv(r, k, l, row, rows):
        s = r % 2
        a, b = (mod, vod) if k == 2 else (mo, vo)
        return (pltpu.make_async_copy(a.at[s], nm[k].at[l, pl.ds(row, rows), :], osem.at[s, 0]),
                pltpu.make_async_copy(b.at[s], nv[k].at[l, pl.ds(row, rows), :], osem.at[s, 1]))
    def own_sent(r):
        def fn(*a):
            c, right, left, other = own_w(r, *a)
            c().wait()
            @pl.when(chip < 3)
            def _(): right().wait_send()
            @pl.when(chip > 0)
            def _(): left().wait_send()
            other().wait_send()
        each(r, fn)
    def own_mv_done(r):
        def fn(*a):
            for c in own_mv(r, *a): c.wait()
        each(r, fn)

    def own(r):
        s = r % 2
        s4 = r % WS
        @pl.when(r + 1 < NM)
        def _(): start_fetch(r + 1)
        forward_done(r + LEAD - 2)
        forward(r + LEAD)
        def fw(*a):
            for c in fetch(r)(*a): c.wait()
        each(r, fw)
        @pl.when(r >= WS)
        def _(): own_sent(r - WS)
        @pl.when(r >= 2)
        def _(): own_mv_done(r - 2)
        lg, mat, rg, ld, rdn = parts(r)
        @pl.when(r < MG)
        def _():
            @pl.when(~end)
            def _():
                rows = pl.ds(pl.multiple_of(rg, 16), GR); cols = pl.ds(pl.multiple_of(mat * BF, 128), BF)
                rdma(guf[0].at[:, 0, rows, cols], ggu.at[lg, :, rows, cols], fgu.at[0], rgu.at[r], me).wait_recv()
            def blk(t, z):
                b, hh = t // (GR // 16), t % (GR // 16)
                c = pl.ds(pl.multiple_of(b * BF, 128), BF)
                rr = pl.ds(pl.multiple_of(hh * 16, 16), 16)
                g = ggu[lg, b, pl.ds(pl.multiple_of(rg + hh * 16, 16), 16), pl.ds(pl.multiple_of(mat * BF, 128), BF)]
                a, bb, cc = adamw(wb[s, rr, c], mb[s, rr, c], vb[s, rr, c], g)
                wo[s4, rr, c] = a; mo[s, rr, c] = bb; vo[s, rr, c] = cc
                return z
            lax.fori_loop(0, NB * (GR // 16), blk, 0)
        @pl.when(r >= MG)
        def _():
            for h in (0, 1):
                @pl.when(~(end & (core == h)))
                def _():
                    rows = pl.ds(pl.multiple_of(rdn, 16), DR)
                    rdma(df[0].at[pl.ds(0, DR), :], gd.at[ld, h, rows, :], fd.at[0, 0], rd.at[r - MG, h], me).wait_recv()
            for h in (0, 1):
                def blk(t, z):
                    rr = pl.ds(pl.multiple_of(t * 16, 16), 16)
                    c = pl.ds(HD * h, HD)
                    g = gd[ld, h, pl.ds(pl.multiple_of(rdn + t * 16, 16), 16), :]
                    a, bb, cc = adamw(wbd[s, rr, c], mbd[s, rr, c], vbd[s, rr, c], g)
                    wod[s4, rr, c] = a; mod[s, rr, c] = bb; vod[s, rr, c] = cc
                    return z
                lax.fori_loop(0, DR // 16, blk, 0)
        def send(*a):
            c, right, left, other = own_w(r, *a)
            @pl.when(chip > 0)
            def _(): left().start()
            @pl.when(chip < 3)
            def _(): right().start()
            other().start()
            c().start()
            for c in own_mv(r, *a): c.start()
        each(r, send)

    def relay_copies(dr, dist, r, k, l, row, rows):
        dev = me + 2 * dist if dr else me - 2 * dist
        ref = place(k, dev, l, row, rows)
        to = me - 2 if dr else me + 2
        return (lambda: rdma(ref, ref, relay_send.at[dr, dist - 1], rsem.at[dr, dist, r], to),
                lambda: rdma(ref, ref, relay_sib.at[dr, dist - 1], sibr.at[k], sib),
                lambda: rdma(ref, ref, relay_send.at[dr, dist - 1], rsem.at[dr, dist - 1, r], to))
    def relay_sent(dr, dist, r, onward):
        def fn(*a):
            on, other, _ = relay_copies(dr, dist, r, *a)
            @pl.when(onward)
            def _(): on().wait_send()
            other().wait_send()
        each(r, fn)
    def relays(r, z):
        for dr in (0, 1):
            def one(dist, zz):
                rr = r - dist
                there = (chip + dist <= 3) if dr else (chip - dist >= 0)
                onward = (chip > 0) if dr else (chip < 3)
                @pl.when(there & (rr >= 0) & (rr < NM))
                def _():
                    @pl.when(rr >= 1)
                    def _(): relay_sent(dr, dist, rr - 1, onward)
                    def fn(*a):
                        on, other, came = relay_copies(dr, dist, rr, *a)
                        came().wait_recv()
                        @pl.when(onward)
                        def _(): on().start()
                        other().start()
                    each(rr, fn)
                    @pl.when(rr == NM - 1)
                    def _(): relay_sent(dr, dist, rr, onward)
                return zz
            lax.fori_loop(1, 4, one, 0)
    def rnd(r, z):
        @pl.when(r < NM)
        def _(): own(r)
        relays(r, z)
        return z
    lax.fori_loop(0, NM + 3, rnd, 0)
    for r in range(NM - WS, NM): own_sent(jnp.int32(r))
    for r in range(NM - 2, NM): own_mv_done(jnp.int32(r))
    for r in range(NM + LEAD - 2, NM): forward_done(jnp.int32(r))
    for k in range(3):
        rdma(nw[k].at[0], nw[k].at[0], wsem.at[0, 0], sibr.at[k], sib).wait_recv()
    @pl.when(end)
    def _():
        for t in range(8):
            @pl.when(me != t)
            def _(): ss_copy(t).wait_send()

def kcall(gu1, gu0, d1, d0, ss, ws, ms, vs):
    V = pl.BlockSpec(memory_space=pltpu.VMEM); A = pl.BlockSpec(memory_space=pl.ANY)
    S = jax.ShapeDtypeStruct
    DMA = pltpu.SemaphoreType.DMA
    outs = [S(w.shape, bf16) for w in ws] + [S(m.shape, f32) for m in ms] * 2
    VM = pltpu.VMEM
    scratch = [VM((2, NB, GRP, 2 * BF), bf16), VM((2, 2, DOWN, HD), bf16),
        VM((2, GR, F), f32), VM((2, GR, F), f32), VM((2, GR, F), bf16), VM((2, GR, F), f32), VM((2, GR, F), f32), VM((WS, GR, F), bf16),
        VM((2, DR, D), f32), VM((2, DR, D), f32), VM((2, DR, D), bf16), VM((2, DR, D), f32), VM((2, DR, D), f32), VM((WS, DR, D), bf16),
        VM((4, 8, 128), f32),
        DMA((4,)), DMA((MG,)), DMA((2 * ND, 2)), DMA((2,)), DMA((4, 2)), DMA((2, 3)), DMA((2, 2)), DMA((WS, 4)), DMA((2, 4, NM)), DMA((2, 3)), DMA((2, 3)), DMA((3,)), DMA((8,)), DMA((4,))]
    return pl.pallas_call(kc_kernel, out_shape=outs, in_specs=[A] * 4 + [V] + [A] * 9, out_specs=[A] * 9, scratch_shapes=scratch, name="gather",
        compiler_params=pltpu.CompilerParams(vmem_limit_bytes=40 << 20, collective_id=2, has_side_effects=True))(
        gu1, gu0, d1.reshape(F // 2, HD), d0.reshape(F // 2, HD), ss, *ws, *ms, *vs)


def solution(mesh):
    def body(x, dy, *arrays):
        weights, m, v = (arrays[i : i + 3] for i in (0, 3, 6))
        x, dy = x[0], dy[0]
        h = ka(x, *weights)
        dh, gu1, d1, ss1 = lcall(h, dy, *weights, layer=1, with_da=True)
        gu0, d0, ss0 = lcall(x, dh, *weights, layer=0, with_da=False)
        return tuple(kcall(gu1, gu0, d1, d0, ss1 + ss0, weights, m, v))

    shard = P(None, "dp", None)
    return jax.shard_map(
        body,
        mesh=mesh,
        in_specs=(P(("rep", "dp")),) * 2 + (P(),) * 3 + (shard,) * 6,
        out_specs=(P("rep"),) * 3 + (P("rep", "dp", None),) * 6,
        check_vma=False,
    )
```

time: 1500 us -> 837 us (0.56)
  waiting for transfers between devices: 925 us -> 0 us
  Pallas kernels: 0 us -> 785 us
  matrix products: 377 us -> 0 us
  other arithmetic: 110 us -> 0.68 us
  between operations: 17.7 us -> 0.74 us
    pallas_call x0 -> x4, Pallas kernels: none -> 785 us  [the longest x2 368 us: lcall(): pl.pallas_call(functools.partial(lkernel, layer=layer, with_da=with_da, c...]
    unnamed x15 -> x0, waiting for transfers between devices: 560 us -> none
    dot_general x15 -> x0, matrix products: 377 us -> none  [the longest x5 131 us: layer(): gate = jnp.dot(a, w['w_gate'], preferred_element_type=jnp.float32)]
    reshape x3 -> x0, waiting for transfers between devices: 365 us -> none  [step(): t.reshape(-1, *t.shape[2:])]
    unnamed x4 -> x1, other arithmetic: 71.5 us -> 0.01 us
    reshape x3 -> x0, other arithmetic: 20.1 us -> none  [step(): t.reshape(-1, *t.shape[2:])]
    unnamed x45 -> x29, local copies, waits for them, and re-layouts: 40.9 us -> 50.5 us
  transfers between devices with their start and end apart: 9 -> 0, of which waited for: 8 -> 0; matrix products, arithmetic and copies ran while one was open for 20% -> 0% of each run, Pallas kernels for 0% -> 0%
where the time goes in v1:
time: 837 us
  Pallas kernels  785 us (94%)
  local copies, waits for them, and re-layouts  50.5 us (6%)
    pallas_call x2, Pallas kernels, lcall(): pl.pallas_call(functools.partial(lkernel, layer=layer, with_da=with_da, c...  368 us
    pallas_call x1, Pallas kernels, kcall(): pl.pallas_call(kc_kernel, out_shape=outs, in_specs=[A] * 4 + [V] + [A] *...  364 us
    pallas_call x1, Pallas kernels, ka(): pl.pallas_call(functools.partial(ka_kernel, layer=layer), out_shape=jax.S...  53.7 us
    unnamed x29, local copies, waits for them, and re-layouts  50.5 us

profile of v1, /device:TPU:0, one launch (start us, length us, event | category | flops | bytes accessed | tf_op | source)
XLA Modules:
  0.0 836.9 jit_solution(17450285925821677343)
XLA Ops:
  0.6 53.7 %ka.1.h_ref = bf16[2048,768]{1,0:T(8,128)(2,1)} custom-call(bf16[2048,768]{1,0:T(8,128)(2,1)} %bitcast.8, bf16[2,768,4480]{2,1,0:T(8,128)(2,1)} %wg.1, bf16[2,768,4480]{2,1,0:T(8,128)(2,1)} %wu.1, bf16[2,4480,768]{2,1,0:T(8,128)(2,1)} %wd.1), custom_call_target="tpu_custom_call" | custom-call | tf_op jit(solution)/shard_map/ka/pallas_call | solution.py:66
  54.4 198.3 %back1.1 = (bf16[2048,768]{1,0:T(8,128)(2,1)}, bf16[7,2,96,1280]{3,2,1,0:T(8,128)(2,1)}, bf16[7,320,384]{2,1,0:T(8,128)(2,1)}, f32[8,128]{1,0:T(8,128)}) custom-call(bf16[2048,768]{1,0:T(8,128)(2,1)} %ka.1.h_ref, bf16[2048,768]{1,0:T(8,128)(2,1)} %bitcast.10, bf16[2,768,4480]{2,1,0:T(8,128)(2,1)} %wg.1, bf16[2,768,4480]{2,1,0:T(8,128)(2,1)} %wu.1, ...), custom_call_target="tpu_custom_call" | custom-call | tf_op jit(solution)/shard_map/back1/pallas_call | solution.py:314
  252.7 0.0 copy-start.5
  252.7 169.2 %back0.1 = (bf16[7,2,96,1280]{3,2,1,0:T(8,128)(2,1)}, bf16[7,320,384]{2,1,0:T(8,128)(2,1)}, f32[8,128]{1,0:T(8,128)}) custom-call(bf16[2048,768]{1,0:T(8,128)(2,1)} %bitcast.9, bf16[2048,768]{1,0:T(8,128)(2,1)} %get-tuple-element.17.dh_ref, bf16[2,768,4480]{2,1,0:T(8,128)(2,1)} %wg.1, bf16[2,768,4480]{2,1,0:T(8,128)(2,1)} %wu.1, bf16[2,4480,768]{2,1,0:T(8,128)(2,1)} %wd.1), custom_call_target="tpu_custom_call" | custom-call | tf_op jit(solution)/shard_map/back0/pallas_call | solution.py:314
  421.9 0.0 copy-done.5
  421.9 0.7 add.3.ss_ref
  422.6 0.0 copy-start
  422.6 1.5 copy-done
  424.1 0.0 copy-start.1
  424.1 1.5 copy-done.1
  425.5 363.6 %gather.1 = (bf16[2,768,4480]{2,1,0:T(8,128)(2,1)}, bf16[2,768,4480]{2,1,0:T(8,128)(2,1)}, bf16[2,4480,768]{2,1,0:T(8,128)(2,1)}, f32[2,96,4480]{2,1,0:T(8,128)S...) custom-call(bf16[7,2,96,1280]{3,2,1,0:T(8,128)(2,1)} %get-tuple-elem, ...), custom_call_target="tpu_custom_call" | custom-call | tf_op jit(solution)/shard_map/gather/pallas_call | solution.py:608
  789.2 0.0 slice-start
  789.2 0.0 slice-start.1
  789.2 0.0 slice-start.2
  789.2 14.7 %copy.29 = bf16[2,768,4480]{2,1,0:T(8,128)(2,1)} copy(bf16[2,768,4480]{2,1,0:T(8,128)(2,1)} %get-tuple-element.32) | data formatting | bytes 27525120
  803.9 0.0 slice-start.3
  803.9 12.8 %copy.30 = bf16[2,768,4480]{2,1,0:T(8,128)(2,1)} copy(bf16[2,768,4480]{2,1,0:T(8,128)(2,1)} %get-tuple-element.33) | data formatting | bytes 27525120
  816.7 0.0 slice-done
  816.7 0.0 slice-done.1
  816.7 0.0 slice-done.2
  816.7 0.0 slice-done.3
  816.7 5.2 copy.31
  821.9 1.8 copy.32
  823.7 1.8 copy.33
  825.4 0.0 copy-start.4
  825.4 1.8 copy.34
  827.2 1.5 copy-done.4
  828.7 0.0 copy-start.3
  828.7 1.8 copy.35
  830.4 1.5 copy-done.3
  831.9 0.0 copy-start.2
  831.9 1.8 copy.36
  833.6 1.5 copy-done.2
  835.1 1.8 copy.37
  (1 shorter events, 0.0 us)
Async XLA Ops:
  252.7 169.2 %copy-start.5 = (f32[8,128]{1,0:T(8,128)S(1)}, f32[8,128]{1,0:T(8,128)}, u32[]{:S(2)}) copy-start(f32[8,128]{1,0:T(8,128)} %get-tuple-element.21) | copy-start | bytes 12292
  422.6 1.5 copy-start
  424.1 1.5 copy-start.1
  789.2 27.6 %slice-start = ((s8[13762560]{0:T(1024)(128)(4,1)}), s8[4194304]{0:T(1024)(128)(4,1)S(1)}, s32[]{:S(2)}) async-start(s8[13762560]{0:T(1024)(128)(4,1)} %bitcast.6), calls=%async_computation | async-start | bytes 8388608
  789.2 27.5 %slice-start.1 = ((s8[13762560]{0:T(1024)(128)(4,1)}), s8[4194304]{0:T(1024)(128)(4,1)S(1)}, s32[]{:S(2)}) async-start(s8[13762560]{0:T(1024)(128)(4,1)} %bitcast.6), calls=%async_computation.1 | async-start | bytes 8388608
  789.2 27.5 %slice-start.2 = ((s8[13762560]{0:T(1024)(128)(4,1)}), s8[4194304]{0:T(1024)(128)(4,1)S(1)}, s32[]{:S(2)}) async-start(s8[13762560]{0:T(1024)(128)(4,1)} %bitcast.6), calls=%async_computation.2 | async-start | bytes 8388608
  803.9 12.8 %slice-start.3 = ((s8[13762560]{0:T(1024)(128)(4,1)}), s8[1179648]{0:T(1024)(128)(4,1)S(1)}, s32[]{:S(2)}) async-start(s8[13762560]{0:T(1024)(128)(4,1)} %bitcast.6), calls=%async_computation.3 | async-start | bytes 2359296
  825.4 3.2 copy-start.4
  828.7 3.2 copy-start.3
  831.9 3.2 copy-start.2
